TPU v7x, 32 devices: a whole 2x2x4 slice. The times are simulated.
32 devices in a mesh: seq: 16 (over z, y, x), tensor: 2 (over core).
Axes of the slice: x: 2, y: 2, z: 4, core: 2. Of those that a mesh axis runs over, the one named last changes fastest.
Arguments:
- hidden: bfloat16 [2, 4096, 8192], P(None, 'seq', 'tensor'), may hold values from -160 to 160
- norm_gain: bfloat16 [8192], P('tensor'), may hold values from 0.25 to 1.75
- value_weight: bfloat16 [8192], P('tensor'), may hold values from -0.0625 to 0.0625
- rewards: float32 [2, 4096], P(None, 'seq'), may hold values from -6 to 6
- done_flags: int32 [2, 4096], P(None, 'seq'), may hold values 0 or 1
- valid_mask: int32 [2, 4096], P('tensor', 'seq'), may hold values 0 or 1
- new_logprob: float32 [2, 4096], P('tensor', 'seq'), may hold values from -1 to 1
- old_logprob: float32 [2, 4096], P('tensor', 'seq'), may hold values from -1 to 1
- discount: float32 [2], replicated, may hold values from 0.9 to 1
- trace_decay: float32 [2], replicated, may hold values from 0.9 to 1
- bootstrap: float32 [2], replicated, may hold values from -5 to 5
Outputs:
- values: float32 [2, 4096], P('tensor', 'seq')
- white_adv: float32 [2, 4096], P('tensor', 'seq')
- token_loss: float32 [2, 4096], P('tensor', 'seq')
- policy_loss: float32 [], replicated
All inputs are finite; a program needn't handle non-finite values. No bound on the sum of `done_flags` or of `valid_mask` on one device may be relied on, other than what follows from the above.
Results may differ from a plain program's by a relative error of at most 0.00035.
Values sent between devices are 32-bit elements; how exact they have to be, the bound alone decides.
A program may use at most 64 MiB of HBM per device.

v0:
```python
import jax
import jax.numpy as jnp
from jax import lax
from jax.sharding import PartitionSpec as P

H = 8192
EPS_NORM = 1e-06
EPS_WHITE = 1e-08
CLIP = 0.2
HIGHEST = lax.Precision.HIGHEST


def compose(earlier, later):
    return (later[0] + later[1] * earlier[0], later[1] * earlier[1])


def local_pass(values, rewards, done_flags, discount, trace_decay):
    row_count, length = values.shape
    alive = 1.0 - done_flags.astype(jnp.float32)
    inner_next = jnp.concatenate([values[:, 1:], jnp.zeros((row_count, 1), jnp.float32)], axis=1)
    delta = rewards + discount[:, None] * alive * inner_next - values
    decay = discount * trace_decay
    counted = jnp.cumsum(done_flags, axis=1) - done_flags
    later_pos = lax.broadcasted_iota(jnp.int32, (length, length), 1)
    early_pos = lax.broadcasted_iota(jnp.int32, (length, length), 0)
    upper = later_pos >= early_pos
    distance = jnp.maximum(later_pos - early_pos, 0).astype(jnp.float32)
    powers = jnp.exp(distance[None, :, :] * jnp.log(decay)[:, None, None])
    same_episode = counted[:, None, :] == counted[:, :, None]
    weights = jnp.where(upper[None, :, :] & same_episode, powers, 0.0)
    local_adv = jnp.einsum(
        "stj,sj->st", weights, delta, precision=HIGHEST, preferred_element_type=jnp.float32
    )
    coef = weights[:, :, length - 1] * (discount * alive[:, length - 1])[:, None]
    return (local_adv, coef)


def fold_step(carry, block):
    return (compose(carry, block), carry)


def shards(
    hidden,
    norm_gain,
    value_weight,
    rewards,
    done_flags,
    valid_mask,
    new_logprob,
    old_logprob,
    discount,
    trace_decay,
    bootstrap,
):
    seqs_all = hidden.shape[0]
    own_rows = seqs_all // lax.axis_size("tensor")
    first_row = lax.axis_index("tensor") * own_rows
    scaled = norm_gain.astype(jnp.float32) * value_weight.astype(jnp.float32)
    squares = jnp.einsum("sth,sth->st", hidden, hidden, preferred_element_type=jnp.float32)
    products = jnp.einsum(
        "sth,h->st", hidden, scaled, precision=HIGHEST, preferred_element_type=jnp.float32
    )
    squares, products = (
        lax.psum_scatter(squares, "tensor", scatter_dimension=0, tiled=True),
        lax.psum_scatter(products, "tensor", scatter_dimension=0, tiled=True),
    )
    values = products * lax.rsqrt(squares / H + EPS_NORM)

    def pick(array):
        return lax.dynamic_slice_in_dim(array, first_row, own_rows, 0)

    rewards_rows = pick(rewards)
    flags_rows = pick(done_flags)
    discount_rows = pick(discount)
    trace_rows = pick(trace_decay)
    local_adv, coef = local_pass(values, rewards_rows, flags_rows, discount_rows, trace_rows)
    weight = valid_mask.astype(jnp.float32)
    offset = values[:, 0] + trace_rows * local_adv[:, 0]
    slope = trace_rows * coef[:, 0]
    packed = jnp.stack(
        [
            offset,
            slope,
            jnp.sum(weight, axis=1),
            jnp.sum(weight * local_adv, axis=1),
            jnp.sum(weight * coef, axis=1),
            jnp.sum(weight * local_adv * local_adv, axis=1),
            jnp.sum(weight * local_adv * coef, axis=1),
            jnp.sum(weight * coef * coef, axis=1),
        ],
        axis=1,
    )
    gathered = lax.all_gather(packed[None], ("seq", "tensor"), axis=0, tiled=True)
    seq_count = lax.axis_size("seq")
    table = gathered.reshape(seq_count, seqs_all, 8)
    start_pair = (jnp.zeros((seqs_all,), jnp.float32), jnp.ones((seqs_all,), jnp.float32))
    _, prefix = lax.scan(fold_step, start_pair, (table[:, :, 0], table[:, :, 1]), reverse=True)
    entering = prefix[0] + prefix[1] * bootstrap[None, :]
    count = jnp.sum(table[:, :, 2])
    total = jnp.sum(table[:, :, 3] + entering * table[:, :, 4])
    square_sum = jnp.sum(
        table[:, :, 5] + 2.0 * entering * table[:, :, 6] + entering * entering * table[:, :, 7]
    )
    mean = total / count
    variance = square_sum / count - mean * mean
    own_entering = lax.dynamic_slice_in_dim(
        lax.dynamic_index_in_dim(entering, lax.axis_index("seq"), 0, False), first_row, own_rows, 0
    )
    adv_own = local_adv + coef * own_entering[:, None]
    white_adv = (adv_own - mean) * lax.rsqrt(variance + EPS_WHITE)
    ratio = jnp.exp(new_logprob - old_logprob)
    surrogate = jnp.minimum(ratio * white_adv, jnp.clip(ratio, 1.0 - CLIP, 1.0 + CLIP) * white_adv)
    token_loss = -weight * surrogate
    loss_sum = lax.psum(jnp.sum(token_loss), ("seq", "tensor"))
    policy_loss = loss_sum / count
    return (values, white_adv, token_loss, policy_loss)


def solution(mesh):
    in_specs = (
        P(None, "seq", "tensor"),
        P("tensor"),
        P("tensor"),
        P(None, "seq"),
        P(None, "seq"),
        P("tensor", "seq"),
        P("tensor", "seq"),
        P("tensor", "seq"),
        P(),
        P(),
        P(),
    )
    out_specs = (P("tensor", "seq"), P("tensor", "seq"), P("tensor", "seq"), P())
    return jax.shard_map(shards, mesh=mesh, in_specs=in_specs, out_specs=out_specs, check_vma=False)
```

profile of v0, /device:TPU:12, one launch (start us, length us, event | category | flops | bytes accessed | tf_op | source)
XLA Modules:
  0.0 122.1 jit_solution(13526523173218547624)
XLA Ops:
  0.6 0.9 convert_multiply_fusion.1
  1.6 6.0 %fusion.45 = f32[1,2,256]{2,0,1:T(1,128)S(1)} fusion(f32[4096,1,1]{0,1,2:T(1,128)S(1)} %bitcast.83, bf16[2,256,4096]{2,1,0:T(8,128)(2,1)} %param.13), kind=kOutput, calls=%fused_computation.75 | convolution fusion | flops 25165824 | bytes 4212736 | tf_op jit(solution)/shard_map/sth,h->st/dot_general | solution.py:60
  7.6 0.9 fusion.3
  8.5 2.5 %all-reduce.2 = (f32[2,256]{1,0:T(2,128)S(1)}, f32[2,256]{1,0:T(2,128)S(1)}) all-reduce(f32[2,256]{1,0:T(2,128)S(1)} %bitcast.85, f32[2,256]{1,0:T(2,128)S(1)} %fusion.3), channel_id=3, replica_groups=mesh['seq'=16,'tensor'=2] {'tensor'}, use_global_device_ids=true, to_apply=%region_0.0.clone | all-reduce | flops 1024 | bytes 8192
  11.0 0.6 dynamic-slice.1
  11.5 0.7 dynamic-slice_multiply_fusion.1
  12.2 0.6 dynamic_slice.37
  12.8 0.6 slice.66
  14.7 0.6 dynamic_slice.38
  16.6 0.3 reduce-window.6
  17.0 0.2 slice_reduce_fusion.1
  17.1 0.2 reduce-window.9
  17.4 0.6 slice.65
  18.1 2.3 %multiply_reduce_fusion = (f32[]{:T(128)}, f32[]{:T(128)}, f32[]{:T(128)}, f32[]{:T(128)}, f32[]{:T(128)}, /*index=5*/f32[]{:T(128)}, f32[1,256,1]{1,2,0:T(1,128)S(1)}, f32[1,256]{1,0:T(1,128)S(1)}) fusion(s32[1,256]{1,0:T(1,128)S(1)} %copy-done.3, f32[]{:T(128)} %bitcast.13, f32[]{:T(128)} %bitcast.7, s32[256]{0:T(256)S(1)} %bitcast.96, s32[1]{0:T(128)} %slice.65, ...), kind=kOutput, calls=%fused_computation.56 | convolution fusion | flops 1318138 | bytes 13340 | tf_op jit(solution)/shard_map/stj,sj->st/dot_general | solution.py:31
  20.4 0.5 slice.67
  20.9 0.5 slice.68
  23.4 0.5 slice.69
  25.2 3.8 %stack.35 = f32[1,8]{1,0:T(1,128)S(1)} concatenate(f32[1,1]{1,0:T(1,128)} %bitcast.16, f32[1,1]{1,0:T(1,128)} %bitcast.19, f32[1,1]{1,0:T(1,128)} %bitcast.20, f32[1,1]{1,0:T(1,128)} %bitcast.21, f32[1,1]{1,0:T(1,128)} %bitcast.22, f32[1,1]{1,0:T(1,128)} %bitcast.23, f32[1,1]{1,0:T(1,128)} %bitcast.24, f32[1,1]{1,0:T(1,128)} %bitcast.25), dimensions={1} | concatenate | bytes 64 | tf_op jit(solution)/shard_map/stack | solution.py:80
  29.0 31.7 %all-gather.1 = f32[32,1,8]{2,1,0:T(1,128)S(1)} all-gather(f32[1,1,8]{2,1,0:T(1,128)S(1)} %bitcast.92), channel_id=2, replica_groups=mesh['seq'=16,'tensor'=2] {'seq','tensor'}, dimensions={0}, use_global_device_ids=true | all-gather | bytes 1056 | tf_op jit(solution)/shard_map/all_gather | solution.py:93
  60.7 0.7 slice_reduce_fusion
  61.4 0.1 copy.56
  61.5 0.1 copy.55
  61.6 0.1 copy.59
  61.7 0.1 copy.58
  61.8 0.1 copy.57
  61.9 0.1 copy.53
  62.3 1.9 %while.21 = (s32[]{:T(128)}, f32[2]{0:T(128)S(1)}, f32[2]{0:T(128)S(1)}, f32[16,2]{1,0:T(8,128)S(1)}, f32[16,2]{1,0:T(8,128)S(1)}, /*index=5*/f32[16,2]{1,0:T(8,...) while((s32[]{:T(128)}, f32[2]{0:T(128)S(1)}, f32[2]{0:T(128)S(1)}, ...), condition=%wide.region_11.12_spmd.clone, body=%wide.region_10.11_spmd.clone.sunk | while | flops 14 | bytes 239 | solution.py:97
  64.3 0.7 fusion.34
  65.0 0.7 dynamic_slice.40
  65.7 0.7 broadcast_multiply_fusion
  69.1 1.3 %fusion.43 = (f32[]{:T(128)}, f32[1,256]{1,0:T(1,128)}) fusion(f32[1,256]{1,0:T(1,128)S(1)} %bitcast.90, f32[1,256]{1,0:T(1,128)S(1)} %copy-done.4, f32[1,256]{1,0:T(1,128)S(1)} %copy-done.5, s32[1,256]{1,0:T(1,128)S(1)} %copy-done.3), kind=kLoop, calls=%fused_computation.74 | loop fusion | flops 2303 | bytes 5124 | tf_op jit(solution)/shard_map/reduce_sum | solution.py:114
  70.4 49.3 %psum.7 = f32[]{:T(128)} all-reduce(f32[]{:T(128)} %get-tuple-element.217), channel_id=1, replica_groups=mesh['seq'=16,'tensor'=2] {'seq','tensor'}, use_global_device_ids=true, to_apply=%region_16.17 | all-reduce | flops 1 | bytes 8 | tf_op jit(solution)/shard_map/psum | solution.py:114
  (88 shorter events, 2.2 us)
Async XLA Ops:
  0.6 6.9 %copy-start = (bf16[2,256,4096]{2,1,0:T(8,128)(2,1)S(1)}, bf16[2,256,4096]{2,1,0:T(8,128)(2,1)}, u32[]{:S(2)}) copy-start(bf16[2,256,4096]{2,1,0:T(8,128)(2,1)} %param.13) | copy-start | bytes 12582916
  1.5 9.4 %copy-start.11 = (u32[32]{0:T(128)S(1)}, u32[32]{0:T(128)}, u32[]{:S(2)}) copy-start(u32[32]{0:T(128)} %constant.101) | copy-start | bytes 388
  1.5 10.7 %copy-start.9 = (f32[2]{0:T(128)S(1)}, f32[2]{0:T(128)}, u32[]{:S(2)}) copy-start(f32[2]{0:T(128)} %param.21) | copy-start | bytes 28
  1.5 11.3 %copy-start.6 = (s32[2,256]{1,0:T(2,128)S(1)}, s32[2,256]{1,0:T(2,128)}, u32[]{:S(2)}) copy-start(s32[2,256]{1,0:T(2,128)} %param.17) | copy-start | bytes 6148
  1.5 13.2 %copy-start.10 = (f32[2]{0:T(128)S(1)}, f32[2]{0:T(128)}, u32[]{:S(2)}) copy-start(f32[2]{0:T(128)} %param.22) | copy-start | bytes 28
  1.5 16.5 %copy-start.3 = (s32[1,256]{1,0:T(1,128)S(1)}, s32[1,256]{1,0:T(1,128)}, u32[]{:S(2)}) copy-start(s32[1,256]{1,0:T(1,128)} %param.18) | copy-start | bytes 3076
  1.5 16.5 %copy-start.8 = (f32[2,256]{1,0:T(2,128)S(1)}, f32[2,256]{1,0:T(2,128)}, u32[]{:S(2)}) copy-start(f32[2,256]{1,0:T(2,128)} %param.16) | copy-start | bytes 6148
  1.6 62.8 %copy-start.7 = (f32[2]{0:T(128)S(1)}, f32[2]{0:T(128)}, u32[]{:S(2)}) copy-start(f32[2]{0:T(128)} %param.23) | copy-start | bytes 28
  1.6 67.5 %copy-start.4 = (f32[1,256]{1,0:T(1,128)S(1)}, f32[1,256]{1,0:T(1,128)}, u32[]{:S(2)}) copy-start(f32[1,256]{1,0:T(1,128)} %param.19) | copy-start | bytes 3076
  1.6 67.5 %copy-start.5 = (f32[1,256]{1,0:T(1,128)S(1)}, f32[1,256]{1,0:T(1,128)}, u32[]{:S(2)}) copy-start(f32[1,256]{1,0:T(1,128)} %param.20) | copy-start | bytes 3076
  12.2 108.8 %copy-start.1 = (f32[1,256]{1,0:T(1,128)}, f32[1,256]{1,0:T(1,128)S(1)}, u32[]{:S(2)}) copy-start(f32[1,256]{1,0:T(1,128)S(1)} %dynamic-slice_multiply_fusion.1) | copy-start | bytes 3076
  69.1 51.9 %copy-start.2 = (f32[256]{0:T(256)}, f32[256]{0:T(256)S(1)}, u32[]{:S(2)}) copy-start(f32[256]{0:T(256)S(1)} %subtract_multiply_fusion) | copy-start | bytes 3076
where the time goes:
time: 123 us; the launch traced here: 122 us
  blocking collectives  83.5 us (68%)
  between operations  11.8 us (10%)
  local copies, waits for them, and re-layouts  11.5 us (9%)
  matrix products  8.29 us (7%)
  other arithmetic  6.61 us (5%)
    psum x1, blocking collectives, shards(): loss_sum = lax.psum(jnp.sum(token_loss), ('seq', 'tensor'))  49.3 us
    all_gather x1, blocking collectives, shards(): lax.all_gather(packed[None], ('seq', 'tensor'), axis=0, tiled=True)  31.7 us
    dot_general x1, matrix products, shards(): jnp.einsum('sth,h->st', hidden, scaled, precision=HIGHEST, preferred_elem...  5.97 us
    another operation x1, local copies, waits for them, and re-layouts, shards(): jnp.stack([offset, slope, jnp.sum(weight, axis=1), jnp.sum(weight * local...  3.84 us
    unnamed x1, blocking collectives  2.47 us

commit v1 on v0

--- a/solution.py
+++ b/solution.py
@@ -90,7 +90,11 @@
         ],
         axis=1,
     )
-    gathered = lax.all_gather(packed[None], ("seq", "tensor"), axis=0, tiled=True)
+    block_2 = packed[None]
+    size = lax.axis_size(("seq", "tensor"))
+    parts = jnp.stack([block_2 for _ in range(size)])
+    parts = lax.all_to_all(parts, ("seq", "tensor"), split_axis=0, concat_axis=0)
+    gathered = jnp.concatenate(parts, axis=0)
     seq_count = lax.axis_size("seq")
     table = gathered.reshape(seq_count, seqs_all, 8)
     start_pair = (jnp.zeros((seqs_all,), jnp.float32), jnp.ones((seqs_all,), jnp.float32))

time: 123 us -> 94.6 us (0.77)
  blocking collectives: 83.5 us -> 43.8 us
  starting transfers between devices: 0 us -> 5.99 us
  waiting for transfers between devices: 0 us -> 5.01 us
  matrix products: 8.29 us -> 5.63 us
  other arithmetic: 6.61 us -> 8.74 us
    all_gather x1 -> x0, blocking collectives: 31.7 us -> none  [shards(): lax.all_gather(packed[None], ('seq', 'tensor'), axis=0, tiled=True)]
    psum x1, blocking collectives: 49.3 us -> 41.3 us  [shards(): loss_sum = lax.psum(jnp.sum(token_loss), ('seq', 'tensor'))]
    all_to_all x0 -> x1, starting transfers between devices: none -> 5.99 us  [shards(): lax.all_to_all(parts, ('seq', 'tensor'), split_axis=0, concat_axis=0)]
    all_to_all x0 -> x1, waiting for transfers between devices: none -> 5.01 us  [shards(): lax.all_to_all(parts, ('seq', 'tensor'), split_axis=0, concat_axis=0)]
    dot_general x1, matrix products: 5.97 us -> 3.34 us  [shards(): jnp.einsum('sth,h->st', hidden, scaled, precision=HIGHEST, preferred_elem...]
    dot_general x1, other arithmetic: 0.91 us -> 3.23 us  [shards(): jnp.einsum('sth,sth->st', hidden, hidden, preferred_element_type=jnp.floa...]
  transfers between devices with their start and end apart: 0 -> 1, of which waited for: 0 -> 1; matrix products, arithmetic and copies ran while one was open for 0% -> 0% of each run, Pallas kernels for 0% -> 0%
where the time goes in v1:
time: 94.6 us; the launch traced here: 93.4 us
  blocking collectives  43.8 us (46%)
  local copies, waits for them, and re-layouts  12.1 us (13%)
  between operations  11.9 us (13%)
  other arithmetic  8.74 us (9%)
  starting transfers between devices  5.99 us (6%)
  matrix products  5.63 us (6%)
  waiting for transfers between devices  5.01 us (5%)
    psum x1, blocking collectives, shards(): loss_sum = lax.psum(jnp.sum(token_loss), ('seq', 'tensor'))  41.3 us
    all_to_all x1, starting transfers between devices, shards(): lax.all_to_all(parts, ('seq', 'tensor'), split_axis=0, concat_axis=0)  5.99 us
    all_to_all x1, waiting for transfers between devices, shards(): lax.all_to_all(parts, ('seq', 'tensor'), split_axis=0, concat_axis=0)  5.01 us
    another operation x1, local copies, waits for them, and re-layouts, shards(): jnp.stack([offset, slope, jnp.sum(weight, axis=1), jnp.sum(weight * local...  3.71 us
    dot_general x1, matrix products, shards(): jnp.einsum('sth,h->st', hidden, scaled, precision=HIGHEST, preferred_elem...  3.34 us
    dot_general x1, other arithmetic, shards(): jnp.einsum('sth,sth->st', hidden, hidden, preferred_element_type=jnp.floa...  3.23 us
    unnamed x1, blocking collectives  2.46 us
    dot_general x1, matrix products, local_pass(): jnp.einsum('stj,sj->st', weights, delta, precision=HIGHEST, preferred_ele...  2.29 us
  transfers between devices with their start and end apart: 1, of which 1 were waited for; matrix products, arithmetic and copies ran while one was open for 0% of the time, Pallas kernels for 0%

profile of v1, /device:TPU:12, one launch (start us, length us, event | category | flops | bytes accessed | tf_op | source)
XLA Modules:
  0.0 93.4 jit_solution(14573664629700112390)
XLA Ops:
  0.8 3.2 %fusion.3 = f32[2,256]{1,0:T(2,128)S(1)} fusion(bf16[2,256,4096]{2,1,0:T(8,128)(2,1)} %param.13), kind=kLoop, calls=%fused_computation.9 | loop fusion | flops 6290944 | bytes 4196352 | tf_op jit(solution)/shard_map/sth,sth->st/dot_general | solution.py:59
  4.0 0.7 convert_multiply_fusion.1
  4.7 3.3 %fusion.45 = f32[1,2,256]{2,0,1:T(1,128)S(1)} fusion(f32[4096,1,1]{0,1,2:T(1,128)S(1)} %bitcast.83, bf16[2,256,4096]{2,1,0:T(8,128)(2,1)S(1)} %copy-done), kind=kOutput, calls=%fused_computation.75 | convolution fusion | flops 25165824 | bytes 4212736 | tf_op jit(solution)/shard_map/sth,h->st/dot_general | solution.py:60
  8.0 2.5 %all-reduce.2 = (f32[2,256]{1,0:T(2,128)S(1)}, f32[2,256]{1,0:T(2,128)S(1)}) all-reduce(f32[2,256]{1,0:T(2,128)S(1)} %bitcast.85, f32[2,256]{1,0:T(2,128)S(1)} %fusion.3), channel_id=2, replica_groups=mesh['seq'=16,'tensor'=2] {'tensor'}, use_global_device_ids=true, to_apply=%region_0.0.clone | all-reduce | flops 1024 | bytes 8192
  10.5 0.6 dynamic-slice.1
  11.1 0.7 dynamic-slice_multiply_fusion.1
  11.8 0.6 slice.67
  12.4 0.6 dynamic_slice.37
  13.0 0.6 slice.66
  13.6 0.6 dynamic_slice.38
  16.8 0.3 reduce-window.6
  17.1 0.2 slice_reduce_fusion.1
  17.3 0.2 reduce-window.9
  17.6 0.6 slice.65
  18.2 2.3 %multiply_reduce_fusion = (f32[]{:T(128)}, f32[]{:T(128)}, f32[]{:T(128)}, f32[]{:T(128)}, f32[]{:T(128)}, /*index=5*/f32[]{:T(128)}, f32[1,256,1]{1,2,0:T(1,128)S(1)}, f32[1,256]{1,0:T(1,128)S(1)}) fusion(s32[1,256]{1,0:T(1,128)S(1)} %copy-done.4, f32[]{:T(128)} %bitcast.13, f32[]{:T(128)} %bitcast.7, s32[256]{0:T(256)S(1)} %bitcast.96, s32[1]{0:T(128)} %slice.65, ...), kind=kOutput, calls=%fused_computation.56 | convolution fusion | flops 1318138 | bytes 13340 | tf_op jit(solution)/shard_map/stj,sj->st/dot_general | solution.py:31
  20.5 0.5 slice.68
  22.3 0.5 slice.69
  24.8 3.7 %stack.40 = f32[1,8]{1,0:T(1,128)S(1)} concatenate(f32[1,1]{1,0:T(1,128)} %bitcast.16, f32[1,1]{1,0:T(1,128)} %bitcast.19, f32[1,1]{1,0:T(1,128)} %bitcast.20, f32[1,1]{1,0:T(1,128)} %bitcast.21, f32[1,1]{1,0:T(1,128)} %bitcast.22, f32[1,1]{1,0:T(1,128)} %bitcast.23, f32[1,1]{1,0:T(1,128)} %bitcast.24, f32[1,1]{1,0:T(1,128)} %bitcast.25), dimensions={1} | concatenate | bytes 64 | tf_op jit(solution)/shard_map/stack | solution.py:80
  28.5 0.6 stack.42
  29.1 6.0 %all-to-all-start = ((f32[32,1,1,8]{3,2,1,0:T(1,128)}), f32[32,1,1,8]{3,2,1,0:T(1,128)S(1)}, u32[]{:S(2)}, u32[]{:S(2)}) async-start(f32[32,1,1,8]{3,2,1,0:T(1,128)} %stack.42), calls=%async_computation | async-start | bytes 32768 | tf_op jit(solution)/shard_map/all_to_all | solution.py:96
  35.1 5.0 %all-to-all-done = f32[32,1,1,8]{3,2,1,0:T(1,128)S(1)} async-done(((f32[32,1,1,8]{3,2,1,0:T(1,128)}), f32[32,1,1,8]{3,2,1,0:T(1,128)S(1)}, u32[]{:S(2)}, u32[]{:S(2)}) %all-to-all-start) | async-done | bytes 1056 | tf_op jit(solution)/shard_map/all_to_all | solution.py:96
  40.1 0.7 slice_reduce_fusion
  40.8 0.1 copy.37
  40.9 0.1 copy.36
  41.0 0.1 copy.40
  41.3 0.1 copy.30
  41.7 1.8 %while.21 = (s32[]{:T(128)}, f32[2]{0:T(128)S(1)}, f32[2]{0:T(128)S(1)}, f32[16,2]{1,0:T(8,128)S(1)}, f32[16,2]{1,0:T(8,128)S(1)}, /*index=5*/f32[16,2]{1,0:T(8,...) while((s32[]{:T(128)}, f32[2]{0:T(128)S(1)}, f32[2]{0:T(128)S(1)}, ...), condition=%wide.region_11.12_spmd.clone, body=%wide.region_10.11_spmd.clone.sunk | while | flops 14 | bytes 239 | solution.py:101
  43.6 0.7 fusion.34
  44.3 0.7 dynamic_slice.40
  45.0 0.7 broadcast_multiply_fusion
  48.4 1.3 %fusion.43 = (f32[]{:T(128)}, f32[1,256]{1,0:T(1,128)}) fusion(f32[1,256]{1,0:T(1,128)S(1)} %bitcast.90, f32[1,256]{1,0:T(1,128)S(1)} %copy-done.5, f32[1,256]{1,0:T(1,128)S(1)} %copy-done.6, s32[1,256]{1,0:T(1,128)S(1)} %copy-done.4), kind=kLoop, calls=%fused_computation.74 | loop fusion | flops 2303 | bytes 5124 | tf_op jit(solution)/shard_map/reduce_sum | solution.py:118
  49.7 41.3 %psum.7 = f32[]{:T(128)} all-reduce(f32[]{:T(128)} %get-tuple-element.217), channel_id=1, replica_groups=mesh['seq'=16,'tensor'=2] {'seq','tensor'}, use_global_device_ids=true, to_apply=%region_16.17 | all-reduce | flops 1 | bytes 8 | tf_op jit(solution)/shard_map/psum | solution.py:118
  (92 shorter events, 2.3 us)
Async XLA Ops:
  0.6 4.1 %copy-start = (bf16[2,256,4096]{2,1,0:T(8,128)(2,1)S(1)}, bf16[2,256,4096]{2,1,0:T(8,128)(2,1)}, u32[]{:S(2)}) copy-start(bf16[2,256,4096]{2,1,0:T(8,128)(2,1)} %param.13) | copy-start | bytes 12582916
  0.6 3.3 %copy-start.1 = (bf16[4096]{0:T(1024)(128)(2,1)S(1)}, bf16[4096]{0:T(1024)(128)(2,1)}, u32[]{:S(2)}) copy-start(bf16[4096]{0:T(1024)(128)(2,1)} %param.15) | copy-start | bytes 24580
  0.7 9.8 %copy-start.12 = (u32[32]{0:T(128)S(1)}, u32[32]{0:T(128)}, u32[]{:S(2)}) copy-start(u32[32]{0:T(128)} %constant.101) | copy-start | bytes 388
  0.7 11.8 %copy-start.10 = (f32[2]{0:T(128)S(1)}, f32[2]{0:T(128)}, u32[]{:S(2)}) copy-start(f32[2]{0:T(128)} %param.21) | copy-start | bytes 28
  0.7 12.3 %copy-start.7 = (s32[2,256]{1,0:T(2,128)S(1)}, s32[2,256]{1,0:T(2,128)}, u32[]{:S(2)}) copy-start(s32[2,256]{1,0:T(2,128)} %param.17) | copy-start | bytes 6148
  0.7 12.9 %copy-start.11 = (f32[2]{0:T(128)S(1)}, f32[2]{0:T(128)}, u32[]{:S(2)}) copy-start(f32[2]{0:T(128)} %param.22) | copy-start | bytes 28
  0.7 17.5 %copy-start.4 = (s32[1,256]{1,0:T(1,128)S(1)}, s32[1,256]{1,0:T(1,128)}, u32[]{:S(2)}) copy-start(s32[1,256]{1,0:T(1,128)} %param.18) | copy-start | bytes 3076
  0.7 17.5 %copy-start.9 = (f32[2,256]{1,0:T(2,128)S(1)}, f32[2,256]{1,0:T(2,128)}, u32[]{:S(2)}) copy-start(f32[2,256]{1,0:T(2,128)} %param.16) | copy-start | bytes 6148
  0.7 42.9 %copy-start.8 = (f32[2]{0:T(128)S(1)}, f32[2]{0:T(128)}, u32[]{:S(2)}) copy-start(f32[2]{0:T(128)} %param.23) | copy-start | bytes 28
  0.7 47.7 %copy-start.5 = (f32[1,256]{1,0:T(1,128)S(1)}, f32[1,256]{1,0:T(1,128)}, u32[]{:S(2)}) copy-start(f32[1,256]{1,0:T(1,128)} %param.19) | copy-start | bytes 3076
  0.7 47.7 %copy-start.6 = (f32[1,256]{1,0:T(1,128)S(1)}, f32[1,256]{1,0:T(1,128)}, u32[]{:S(2)}) copy-start(f32[1,256]{1,0:T(1,128)} %param.20) | copy-start | bytes 3076
  11.8 80.5 %copy-start.2 = (f32[1,256]{1,0:T(1,128)}, f32[1,256]{1,0:T(1,128)S(1)}, u32[]{:S(2)}) copy-start(f32[1,256]{1,0:T(1,128)S(1)} %dynamic-slice_multiply_fusion.1) | copy-start | bytes 3076
  29.1 11.0 %all-to-all-start = ((f32[32,1,1,8]{3,2,1,0:T(1,128)}), f32[32,1,1,8]{3,2,1,0:T(1,128)S(1)}, u32[]{:S(2)}, u32[]{:S(2)}) async-start(f32[32,1,1,8]{3,2,1,0:T(1,128)} %stack.42), calls=%async_computation | async-start | bytes 32768 | tf_op jit(solution)/shard_map/all_to_all | solution.py:96
  48.4 43.9 %copy-start.3 = (f32[256]{0:T(256)}, f32[256]{0:T(256)S(1)}, u32[]{:S(2)}) copy-start(f32[256]{0:T(256)S(1)} %subtract_multiply_fusion) | copy-start | bytes 3076
